TPU v7x, 256 devices: a whole 4x4x8 slice. The times are simulated.
256 devices in a mesh: frames: 16 (over x_hi, z), rows: 16 (over y, x_lo, core).
Axes of the slice: x: 4 (x_hi: 2, x_lo: 2; x = x_hi * 2 + x_lo), y: 4, z: 8, core: 2. Of those that a mesh axis runs over, the one named last changes fastest.
Arguments:
- video: bfloat16 [32, 32, 128, 256], P('frames', 'rows'), may hold values from -6 to 6
- norm_a: float32 [256], replicated, may hold values from 0.5 to 2
- conv_a: bfloat16 [3, 3, 3, 256, 256], replicated, may hold values from -0.078125 to 0.078125
- norm_b: float32 [256], replicated, may hold values from 0.5 to 2
- conv_b: bfloat16 [3, 3, 3, 256, 256], replicated, may hold values from -0.078125 to 0.078125
- norm_c: float32 [256], replicated, may hold values from 0.5 to 2
- w_query: bfloat16 [256, 256], replicated, may hold values from -2 to 2
- w_key: bfloat16 [256, 256], replicated, may hold values from -2 to 2
- w_value: bfloat16 [256, 256], replicated, may hold values from -0.375 to 0.375
- w_out: bfloat16 [256, 256], replicated, may hold values from -0.375 to 0.375
Outputs:
- encoded: bfloat16 [32, 32, 128, 256], P('frames', 'rows')
All inputs are finite; a program needn't handle non-finite values.
Results may differ from a plain program's by a relative error of at most 0.015.
Values may be sent and summed in bfloat16 or wider, within the bound.
A program may use at most 64 MiB of HBM per device.

v0:
```python
import jax
import jax.numpy as jnp
from jax import lax
from jax.sharding import PartitionSpec as P

HEADS = 8


def from_behind(block, axis, distance):
    devices = range(lax.axis_size(axis))
    route = [(i - distance, i) for i in devices if i - distance in devices]
    return lax.ppermute(block, axis, route)


def with_halo(block, sides, width):
    for axis, dim in sides:
        count = lax.axis_size(axis)
        forward = [(i, i + 1) for i in range(count - 1)]
        backward = [(target, source) for source, target in forward]
        low = lax.ppermute(
            lax.slice_in_dim(block, block.shape[dim] - width, None, axis=dim), axis, forward
        )
        high = lax.ppermute(lax.slice_in_dim(block, 0, width, axis=dim), axis, backward)
        block = jnp.concatenate([low, block, high], axis=dim)
    return block


def norm_scale(values, gain):
    floats = values.astype(jnp.float32)
    mean_sq = jnp.mean(floats * floats, axis=-1, keepdims=True)
    return floats * lax.rsqrt(mean_sq + 1e-06) * gain


def apply_kernel(extended, kernel, frames_here, rows_here, width_here):
    channels = extended.shape[-1]
    total = jnp.zeros((frames_here * rows_here * width_here, kernel.shape[-1]), jnp.float32)
    for lag_time in range(3):
        for row_step in range(3):
            for col_step in range(3):
                slab = extended[
                    lag_time : lag_time + frames_here,
                    row_step : row_step + rows_here,
                    col_step : col_step + width_here,
                ]
                total = total + jnp.dot(
                    slab.reshape(-1, channels),
                    kernel[lag_time, row_step, col_step],
                    preferred_element_type=jnp.float32,
                )
    return total.reshape(frames_here, rows_here, width_here, -1)


def causal_conv(active, kernel):
    frames_here, rows_here, width_here, channels = active.shape
    prior = from_behind(active, "frames", 1)
    extended = jnp.concatenate([prior, active], axis=0)
    extended = with_halo(extended, (("rows", 1),), 1)
    extended = jnp.pad(extended, ((0, 0), (0, 0), (1, 1), (0, 0)))
    return apply_kernel(extended, kernel, frames_here, rows_here, width_here)


def project(values, weight):
    return jnp.dot(values, weight, preferred_element_type=jnp.float32).astype(jnp.bfloat16)


def attend(query, keyed, valued):
    frames_all, single, pixels, channels = query.shape
    head_dim = channels // HEADS
    shape4 = (frames_all, pixels, HEADS, head_dim)
    query = query.reshape(shape4)
    keyed = keyed.reshape(shape4)
    valued = valued.reshape(shape4)
    scores = jnp.einsum(
        "tphd,sphd->phts", query, keyed, preferred_element_type=jnp.float32
    ) * head_dim ** (-0.5)
    later = lax.broadcasted_iota(jnp.int32, (frames_all, frames_all), 0)
    earlier = lax.broadcasted_iota(jnp.int32, (frames_all, frames_all), 1)
    scores = jnp.where(later >= earlier, scores, -1e30)
    top = jnp.max(scores, axis=-1, keepdims=True)
    expd = jnp.exp(scores - top)
    probs = (expd / jnp.sum(expd, axis=-1, keepdims=True)).astype(jnp.bfloat16)
    attended = jnp.einsum(
        "phts,sphd->tphd", probs, valued, preferred_element_type=jnp.float32
    ).astype(jnp.bfloat16)
    return attended.reshape(frames_all, single, pixels, channels)


def residual_block(video, norm_a, conv_a, norm_b, conv_b, conv_fn):
    act_a = jax.nn.silu(norm_scale(video, norm_a)).astype(jnp.bfloat16)
    inner = conv_fn(act_a, conv_a).astype(jnp.bfloat16)
    act_b = jax.nn.silu(norm_scale(inner, norm_b)).astype(jnp.bfloat16)
    return (video.astype(jnp.float32) + conv_fn(act_b, conv_b)).astype(jnp.bfloat16)


def shards(video, norm_a, conv_a, norm_b, conv_b, norm_c, w_query, w_key, w_value, w_out):
    block = residual_block(video, norm_a, conv_a, norm_b, conv_b, causal_conv)
    normed = norm_scale(block, norm_c).astype(jnp.bfloat16)
    frames_here, rows_here, width_here, channels = block.shape
    groups = lax.axis_size("frames")
    flat = normed.reshape(frames_here, groups, -1, channels)
    features = lax.all_to_all(flat, "frames", split_axis=1, concat_axis=0, tiled=True)
    result = attend(
        project(features, w_query), project(features, w_key), project(features, w_value)
    )
    moved = project(result, w_out)
    returned = lax.all_to_all(moved, "frames", split_axis=0, concat_axis=1, tiled=True)
    projected = returned
    projected = projected.reshape(block.shape)
    return (block.astype(jnp.float32) + projected.astype(jnp.float32)).astype(jnp.bfloat16)


def solution(mesh):
    placed = (P("frames", "rows", None, None), P(), P(), P(), P(), P(), P(), P(), P(), P())
    return jax.shard_map(
        shards,
        mesh=mesh,
        in_specs=placed,
        out_specs=P("frames", "rows", None, None),
        check_vma=False,
    )
```

profile of v0, /device:TPU:8, one launch (start us, length us, event | category | flops | bytes accessed | tf_op | source)
XLA Modules:
  0.0 115.6 jit_solution(5947308030532247145)
XLA Ops:
  0.0 1.1 fusion.27
  1.2 1.2 %fusion.34 = bf16[2,2,128,256]{3,2,1,0:T(8,128)(2,1)S(1)} fusion(bf16[2,2,128,256]{3,2,1,0:T(8,128)(2,1)} %param.10, f32[256]{0:T(256)} %param.11, f32[2,2,128]{2,1,0:T(2,128)S(1)} %add_rsqrt_fusion.2), kind=kLoop, calls=%fused_computation.112 | loop fusion | flops 1048576 | bytes 527360 | tf_op jit(solution)/shard_map/convert_element_type | solution.py:89
  2.3 3.8 %collective-permute-start = (bf16[2,2,128,256]{3,2,1,0:T(8,128)(2,1)S(1)}, bf16[2,2,128,256]{3,2,1,0:T(8,128)(2,1)S(1)}, u32[]{:S(2)}, u32[]{:S(2)}) collective-permute-start(bf16[2,2,128,256]{3,2,1,0:T(8,128)(2,1)S(1)} %fusion.34), channel_id=1, source_target_pairs={{0,16},{16,32},{32,48},{48,64},{64,80},{80,96},{96,112},{112,128},... | collective-permute-start | bytes 786440 | tf_op jit(solution)/shard_map/ppermute | solution.py:12
  6.2 5.5 %collective-permute-done = bf16[2,2,128,256]{3,2,1,0:T(8,128)(2,1)S(1)} collective-permute-done((bf16[2,2,128,256]{3,2,1,0:T(8,128)(2,1)S(1)}, bf16[2,2,128,256]{3,2,1,0:T(8,128)(2,1)S(1)}, u32[]{:S(2)}, u32[]{:S(2)}) %collective-permute-start) | collective-permute-done | bytes 262176 | tf_op jit(solution)/shard_map/ppermute | solution.py:12
  11.8 1.9 %collective-permute-start.1 = (bf16[4,1,128,256]{3,2,1,0:T(8,128)(2,1)S(1)}, bf16[4,1,128,256]{3,2,1,0:T(8,128)(2,1)S(1)}, u32[]{:S(2)}, u32[]{:S(2)}) collective-permute-start(bf16[4,1,128,256]{3,2,1,0:T(8,128)(2,1)S(1)} %get-tuple-element.61), channel_id=1, source_target_pairs={{0,1},{1,2},{2,3},{3,4},{4,5},{5,6},{6,7},{7,8},{8,9},{9,10},{10,1... | collective-permute-start | bytes 786440 | tf_op jit(solution)/shard_map/ppermute | solution.py:20
  13.7 4.5 %collective-permute-start.2 = (bf16[4,1,128,256]{3,2,1,0:T(8,128)(2,1)S(1)}, bf16[4,1,128,256]{3,2,1,0:T(8,128)(2,1)S(1)}, u32[]{:S(2)}, u32[]{:S(2)}) collective-permute-start(bf16[4,1,128,256]{3,2,1,0:T(8,128)(2,1)S(1)} %get-tuple-element.62), channel_id=1, source_target_pairs={{1,0},{2,1},{3,2},{4,3},{5,4},{6,5},{7,6},{8,7},{9,8},{10,9},{11,1... | collective-permute-start | bytes 786440 | tf_op jit(solution)/shard_map/ppermute | solution.py:23
  18.3 2.2 %collective-permute-done.1 = bf16[4,1,128,256]{3,2,1,0:T(8,128)(2,1)S(1)} collective-permute-done((bf16[4,1,128,256]{3,2,1,0:T(8,128)(2,1)S(1)}, bf16[4,1,128,256]{3,2,1,0:T(8,128)(2,1)S(1)}, u32[]{:S(2)}, u32[]{:S(2)}) %collective-permute-start.1) | collective-permute-done | bytes 262176 | tf_op jit(solution)/shard_map/ppermute | solution.py:20
  20.5 1.6 %collective-permute-done.2 = bf16[4,1,128,256]{3,2,1,0:T(8,128)(2,1)S(1)} collective-permute-done((bf16[4,1,128,256]{3,2,1,0:T(8,128)(2,1)S(1)}, bf16[4,1,128,256]{3,2,1,0:T(8,128)(2,1)S(1)}, u32[]{:S(2)}, u32[]{:S(2)}) %collective-permute-start.2) | collective-permute-done | bytes 262176 | tf_op jit(solution)/shard_map/ppermute | solution.py:23
  22.5 0.8 fusion.182
  23.4 1.1 copy-done.1
  31.4 4.4 %collective-permute-start.3 = (bf16[2,2,128,256]{3,2,1,0:T(8,128)(2,1)S(1)}, bf16[2,2,128,256]{3,2,1,0:T(8,128)(2,1)S(1)}, u32[]{:S(2)}, u32[]{:S(2)}) collective-permute-start(bf16[2,2,128,256]{3,2,1,0:T(8,128)(2,1)S(1)} %multiply_convert_fusion.1), channel_id=1, source_target_pairs={{0,16},{16,32},{32,48},{48,64},{64,80},{80,96},{96,112},{112,128},... | collective-permute-start | bytes 786440 | tf_op jit(solution)/shard_map/ppermute | solution.py:12
  35.8 6.6 %collective-permute-done.3 = bf16[2,2,128,256]{3,2,1,0:T(8,128)(2,1)S(1)} collective-permute-done((bf16[2,2,128,256]{3,2,1,0:T(8,128)(2,1)S(1)}, bf16[2,2,128,256]{3,2,1,0:T(8,128)(2,1)S(1)}, u32[]{:S(2)}, u32[]{:S(2)}) %collective-permute-start.3) | collective-permute-done | bytes 262176 | tf_op jit(solution)/shard_map/ppermute | solution.py:12
  42.5 2.1 %collective-permute-start.4 = (bf16[4,1,128,256]{3,2,1,0:T(8,128)(2,1)S(1)}, bf16[4,1,128,256]{3,2,1,0:T(8,128)(2,1)S(1)}, u32[]{:S(2)}, u32[]{:S(2)}) collective-permute-start(bf16[4,1,128,256]{3,2,1,0:T(8,128)(2,1)S(1)} %get-tuple-element.57), channel_id=1, source_target_pairs={{0,1},{1,2},{2,3},{3,4},{4,5},{5,6},{6,7},{7,8},{8,9},{9,10},{10,1... | collective-permute-start | bytes 786440 | tf_op jit(solution)/shard_map/ppermute | solution.py:20
  44.6 4.3 %collective-permute-start.5 = (bf16[4,1,128,256]{3,2,1,0:T(8,128)(2,1)S(1)}, bf16[4,1,128,256]{3,2,1,0:T(8,128)(2,1)S(1)}, u32[]{:S(2)}, u32[]{:S(2)}) collective-permute-start(bf16[4,1,128,256]{3,2,1,0:T(8,128)(2,1)S(1)} %get-tuple-element.58), channel_id=1, source_target_pairs={{1,0},{2,1},{3,2},{4,3},{5,4},{6,5},{7,6},{8,7},{9,8},{10,9},{11,1... | collective-permute-start | bytes 786440 | tf_op jit(solution)/shard_map/ppermute | solution.py:23
  49.0 7.3 %collective-permute-done.4 = bf16[4,1,128,256]{3,2,1,0:T(8,128)(2,1)S(1)} collective-permute-done((bf16[4,1,128,256]{3,2,1,0:T(8,128)(2,1)S(1)}, bf16[4,1,128,256]{3,2,1,0:T(8,128)(2,1)S(1)}, u32[]{:S(2)}, u32[]{:S(2)}) %collective-permute-start.4) | collective-permute-done | bytes 262176 | tf_op jit(solution)/shard_map/ppermute | solution.py:20
  56.9 0.8 fusion.181
  57.8 1.1 copy-done.2
  66.5 11.3 %all-to-all-start = ((bf16[2,16,16,256]{3,2,0,1:T(8,128)(2,1)}), bf16[2,16,16,256]{3,2,0,1:T(8,128)(2,1)S(1)}, u32[]{:S(2)}, u32[]{:S(2)}) async-start(bf16[2,16,16,256]{3,2,0,1:T(8,128)(2,1)} %copy.18), calls=%async_computation | async-start | bytes 524288 | tf_op jit(solution)/shard_map/all_to_all | solution.py:101
  77.9 11.9 %all-to-all-done = bf16[2,16,16,256]{3,2,0,1:T(8,128)(2,1)S(1)} async-done(((bf16[2,16,16,256]{3,2,0,1:T(8,128)(2,1)}), bf16[2,16,16,256]{3,2,0,1:T(8,128)(2,1)S(1)}, u32[]{:S(2)}, u32[]{:S(2)}) %all-to-all-start) | async-done | bytes 262176 | tf_op jit(solution)/shard_map/all_to_all | solution.py:101
  91.4 1.4 %copy.27 = bf16[32,16,256]{0,2,1:T(8,128)(2,1)} copy(bf16[32,16,256]{2,1,0:T(8,128)(2,1)S(1)} %convolution_convert_fusion.4) | data formatting | bytes 524288 | tf_op jit(solution)/shard_map/reshape | solution.py:72
  92.7 3.3 %fusion.187 = (f32[16,8,32]{2,1,0:T(8,128)S(1)}, f32[16,8,32,32]{2,3,1,0:T(8,128)}) fusion(pred[32,32]{0,1:T(8,128)(4,1)S(1)} %iota_compare_fusion.2, bf16[32,16,8,32]{3,2,1,0:T(8,128)(2,1)S(1)} %reshape.306, bf16[32,16,8,32]{3,2,1,0:T(8,128)(2,1)S(1)} %reshape.305), kind=kOutput, calls=%fused_computation.262 | convolution fusion | flops 8912927 | bytes 1065984 | tf_op jit(solution)/shard_map/sub | solution.py:80
  96.0 2.4 %convolution_convert_fusion = bf16[16,8,32,32]{3,2,1,0:T(8,128)(2,1)S(1)} fusion(bf16[32,16,8,32]{0,3,2,1:T(8,128)(2,1)} %bitcast.326, f32[16,8,32,32]{2,3,1,0:T(8,128)} %get-tuple-element.66, f32[16,8,32]{2,1,0:T(8,128)S(1)} %get-tuple-element.65), kind=kOutput, calls=%fused_computation.8 | convolution fusion | flops 8781824 | bytes 1064960 | tf_op jit(solution)/shard_map/phts,sphd->tphd/dot_general | solution.py:82
  99.1 15.6 %all_to_all.24 = bf16[32,1,16,256]{3,2,1,0:T(8,128)(2,1)S(1)} all-to-all(bf16[32,1,16,256]{3,2,1,0:T(8,128)(2,1)S(1)} %fusion.9), channel_id=1, replica_groups=mesh['frames'=16,'rows'=16] {'frames'}, dimensions={0} | all-to-all | bytes 524288 | tf_op jit(solution)/shard_map/all_to_all | solution.py:106
  114.8 0.8 fusion.39
  (99 shorter events, 17.6 us)
Async XLA Ops:
  0.0 89.8 %copy-start = (bf16[256,256]{1,0:T(8,128)(2,1)S(1)}, bf16[256,256]{1,0:T(8,128)(2,1)}, u32[]{:S(2)}) copy-start(bf16[256,256]{1,0:T(8,128)(2,1)} %param.16) | copy-start | bytes 393220
  2.3 9.4 %collective-permute-start = (bf16[2,2,128,256]{3,2,1,0:T(8,128)(2,1)S(1)}, bf16[2,2,128,256]{3,2,1,0:T(8,128)(2,1)S(1)}, u32[]{:S(2)}, u32[]{:S(2)}) collective-permute-start(bf16[2,2,128,256]{3,2,1,0:T(8,128)(2,1)S(1)} %fusion.34), channel_id=1, source_target_pairs={{0,16},{16,32},{32,48},{48,64},{64,80},{80,96},{96,112},{112,128},... | collective-permute-start | bytes 786440 | tf_op jit(solution)/shard_map/ppermute | solution.py:12
  11.8 8.7 %collective-permute-start.1 = (bf16[4,1,128,256]{3,2,1,0:T(8,128)(2,1)S(1)}, bf16[4,1,128,256]{3,2,1,0:T(8,128)(2,1)S(1)}, u32[]{:S(2)}, u32[]{:S(2)}) collective-permute-start(bf16[4,1,128,256]{3,2,1,0:T(8,128)(2,1)S(1)} %get-tuple-element.61), channel_id=1, source_target_pairs={{0,1},{1,2},{2,3},{3,4},{4,5},{5,6},{6,7},{7,8},{8,9},{9,10},{10,1... | collective-permute-start | bytes 786440 | tf_op jit(solution)/shard_map/ppermute | solution.py:20
  13.7 8.4 %collective-permute-start.2 = (bf16[4,1,128,256]{3,2,1,0:T(8,128)(2,1)S(1)}, bf16[4,1,128,256]{3,2,1,0:T(8,128)(2,1)S(1)}, u32[]{:S(2)}, u32[]{:S(2)}) collective-permute-start(bf16[4,1,128,256]{3,2,1,0:T(8,128)(2,1)S(1)} %get-tuple-element.62), channel_id=1, source_target_pairs={{1,0},{2,1},{3,2},{4,3},{5,4},{6,5},{7,6},{8,7},{9,8},{10,9},{11,1... | collective-permute-start | bytes 786440 | tf_op jit(solution)/shard_map/ppermute | solution.py:23
  22.5 2.0 %copy-start.1 = (bf16[3,3,3,256,256]{4,3,2,1,0:T(8,128)(2,1)S(1)}, bf16[3,3,3,256,256]{4,3,2,1,0:T(8,128)(2,1)}, u32[]{:S(2)}) copy-start(bf16[3,3,3,256,256]{4,3,2,1,0:T(8,128)(2,1)} %param.12) | copy-start | bytes 10616836
  29.9 1.3 %copy-start.7 = (f32[256]{0:T(256)S(1)}, f32[256]{0:T(256)}, u32[]{:S(2)}) copy-start(f32[256]{0:T(256)} %param.13) | copy-start | bytes 3076
  31.4 11.0 %collective-permute-start.3 = (bf16[2,2,128,256]{3,2,1,0:T(8,128)(2,1)S(1)}, bf16[2,2,128,256]{3,2,1,0:T(8,128)(2,1)S(1)}, u32[]{:S(2)}, u32[]{:S(2)}) collective-permute-start(bf16[2,2,128,256]{3,2,1,0:T(8,128)(2,1)S(1)} %multiply_convert_fusion.1), channel_id=1, source_target_pairs={{0,16},{16,32},{32,48},{48,64},{64,80},{80,96},{96,112},{112,128},... | collective-permute-start | bytes 786440 | tf_op jit(solution)/shard_map/ppermute | solution.py:12
  42.5 13.8 %collective-permute-start.4 = (bf16[4,1,128,256]{3,2,1,0:T(8,128)(2,1)S(1)}, bf16[4,1,128,256]{3,2,1,0:T(8,128)(2,1)S(1)}, u32[]{:S(2)}, u32[]{:S(2)}) collective-permute-start(bf16[4,1,128,256]{3,2,1,0:T(8,128)(2,1)S(1)} %get-tuple-element.57), channel_id=1, source_target_pairs={{0,1},{1,2},{2,3},{3,4},{4,5},{5,6},{6,7},{7,8},{8,9},{9,10},{10,1... | collective-permute-start | bytes 786440 | tf_op jit(solution)/shard_map/ppermute | solution.py:20
  44.6 11.7 %collective-permute-start.5 = (bf16[4,1,128,256]{3,2,1,0:T(8,128)(2,1)S(1)}, bf16[4,1,128,256]{3,2,1,0:T(8,128)(2,1)S(1)}, u32[]{:S(2)}, u32[]{:S(2)}) collective-permute-start(bf16[4,1,128,256]{3,2,1,0:T(8,128)(2,1)S(1)} %get-tuple-element.58), channel_id=1, source_target_pairs={{1,0},{2,1},{3,2},{4,3},{5,4},{6,5},{7,6},{8,7},{9,8},{10,9},{11,1... | collective-permute-start | bytes 786440 | tf_op jit(solution)/shard_map/ppermute | solution.py:23
  56.9 2.0 %copy-start.2 = (bf16[3,3,3,256,256]{4,3,2,1,0:T(8,128)(2,1)S(1)}, bf16[3,3,3,256,256]{4,3,2,1,0:T(8,128)(2,1)}, u32[]{:S(2)}) copy-start(bf16[3,3,3,256,256]{4,3,2,1,0:T(8,128)(2,1)} %param.14) | copy-start | bytes 10616836
  64.5 1.0 copy-start.3
  64.5 1.1 copy-start.8
  65.0 25.5 %copy-start.4 = (bf16[256,256]{1,0:T(8,128)(2,1)S(1)}, bf16[256,256]{1,0:T(8,128)(2,1)}, u32[]{:S(2)}) copy-start(bf16[256,256]{1,0:T(8,128)(2,1)} %param.17) | copy-start | bytes 393220
  65.5 25.7 %copy-start.5 = (bf16[256,256]{1,0:T(8,128)(2,1)S(1)}, bf16[256,256]{1,0:T(8,128)(2,1)}, u32[]{:S(2)}) copy-start(bf16[256,256]{1,0:T(8,128)(2,1)} %param.18) | copy-start | bytes 393220
  66.5 23.2 %all-to-all-start = ((bf16[2,16,16,256]{3,2,0,1:T(8,128)(2,1)}), bf16[2,16,16,256]{3,2,0,1:T(8,128)(2,1)S(1)}, u32[]{:S(2)}, u32[]{:S(2)}) async-start(bf16[2,16,16,256]{3,2,0,1:T(8,128)(2,1)} %copy.18), calls=%async_computation | async-start | bytes 524288 | tf_op jit(solution)/shard_map/all_to_all | solution.py:101
  96.0 2.9 %copy-start.6 = (bf16[256,256]{1,0:T(8,128)(2,1)S(1)}, bf16[256,256]{1,0:T(8,128)(2,1)}, u32[]{:S(2)}) copy-start(bf16[256,256]{1,0:T(8,128)(2,1)} %param.19) | copy-start | bytes 393220
where the time goes:
time: 116 us
  waiting for transfers between devices  35.2 us (30%)
  starting transfers between devices  32.5 us (28%)
  matrix products  18.9 us (16%)
  blocking collectives  15.6 us (13%)
  local copies, waits for them, and re-layouts  7.81 us (7%)
  other arithmetic  4.86 us (4%)
    all_to_all x1, blocking collectives, shards(): lax.all_to_all(moved, 'frames', split_axis=0, concat_axis=1, tiled=True)  15.6 us
    dot_general x54, matrix products, apply_kernel(): jnp.dot(slab.reshape(-1, channels), kernel[lag_time, row_step, col_step],...  12.4 us
    ppermute x2, waiting for transfers between devices, from_behind(): return lax.ppermute(block, axis, route)  12.1 us
    all_to_all x1, waiting for transfers between devices, shards(): lax.all_to_all(flat, 'frames', split_axis=1, concat_axis=0, tiled=True)  11.9 us
    all_to_all x1, starting transfers between devices, shards(): lax.all_to_all(flat, 'frames', split_axis=1, concat_axis=0, tiled=True)  11.3 us
    ppermute x2, waiting for transfers between devices, with_halo(): lax.ppermute(lax.slice_in_dim(block, block.shape[dim] - width, None, axis...  9.52 us
    ppermute x2, starting transfers between devices, with_halo(): lax.ppermute(lax.slice_in_dim(block, 0, width, axis=dim), axis, backward)  8.88 us
    ppermute x2, starting transfers between devices, from_behind(): return lax.ppermute(block, axis, route)  8.21 us
  transfers between devices with their start and end apart: 7, of which 6 were waited for; matrix products, arithmetic and copies ran while one was open for 0% of the time, Pallas kernels for 0%

commit v1 on v0

v1 whole, which is shorter than its diff:
```python
import functools

import jax
import jax.numpy as jnp
from jax import lax
from jax.experimental import pallas as pl
from jax.experimental.pallas import tpu as pltpu
from jax.sharding import PartitionSpec as P

MESH = pl.DeviceIdType.MESH
HEADS = 8
C = 256
T = 32
F = 16
R = 16
PATCH = 8
BF = jnp.bfloat16
F32 = jnp.float32


def snake(i):
    half = i // 8
    return i + half * (23 - 2 * i)


def rms(x, gain):
    ms = jnp.mean(x * x, axis=-1, keepdims=True)
    return x * lax.rsqrt(ms + 1e-06) * gain


def silu(x):
    h = 0.5 * x
    return h + h * jnp.tanh(h)


def dot(a, b):
    return jnp.dot(a, b, preferred_element_type=F32)


def dot_tt(a, b, dims):
    return lax.dot_general(a, b, (dims, ((), ())), preferred_element_type=F32)


def shift_rows(y, by):
    rolled = pltpu.roll(y, by, 0)
    frame = lax.broadcasted_iota(jnp.int32, y.shape, 0) % T
    return jnp.where(frame >= by, rolled, 0.0)


def conv_rows(act, kern, row):
    parts = []
    for i in range(3):
        total = None
        for j in range(3):
            for l in range(3):
                slab = act[row + j, l : l + PATCH].reshape(PATCH * T, C)
                term = dot(slab, kern[i * 9 + j * 3 + l])
                total = term if total is None else total + term
        parts.append(total)
    return parts[2] + shift_rows(parts[1], 1) + shift_rows(parts[0], 2)


def one_hot(rows_to):
    a = lax.broadcasted_iota(jnp.int32, (512, 512), 0)
    b = lax.broadcasted_iota(jnp.int32, (512, 512), 1)
    return jnp.where(b == rows_to(a), 1.0, 0.0).astype(BF)


def attend_pixel(q, k, v):
    halves = []
    lane_head = lax.broadcasted_iota(jnp.int32, (T, 128), 1) // 32
    s_at = lax.broadcasted_iota(jnp.int32, (T, 128), 0)
    t_at = lax.broadcasted_iota(jnp.int32, (T, 128), 1) % 32
    for hh in range(2):
        lanes = slice(128 * hh, 128 * hh + 128)
        qh, kh, vh = q[:, lanes], k[:, lanes], v[:, lanes]
        blocks = [jnp.where(lane_head == h, qh.astype(F32), 0.0).astype(BF) for h in range(4)]
        q_bd = jnp.concatenate(blocks, axis=0)
        s = dot_tt(kh, q_bd, ((1,), (1,))) * (32 ** -0.5)
        s = jnp.where(s_at <= t_at, s, -1e30)
        e = jnp.exp(s - jnp.max(s, axis=0, keepdims=True))
        p = (e / jnp.sum(e, axis=0, keepdims=True)).astype(BF)
        o = dot_tt(p, vh, ((0,), (0,)))
        att = jnp.zeros((T, 128), F32)
        for h in range(4):
            att = jnp.where(lane_head == h, o[32 * h : 32 * h + 32], att)
        halves.append(att.astype(BF))
    return halves


def kernel(video, na, ca, nb, cb, nc, wq, wk, wv, wo, out,
           vloc, rin, xres, act_a, act_b, ka, kb, ga, gb, gc, sq, sk, sv, so,
           fwd, bwd, qs, ks, vs, att, blk, sbuf,
           lsem, in_send, in_recv, ha_send, ha_recv, hb_send, hb_recv, out_send, out_recv):
    f = lax.axis_index("frames")
    r = lax.axis_index("rows")
    g = snake(f)
    up, down = (r + R - 1) % R, (r + 1) % R
    west, east = snake((g + F - 1) % F), snake((g + 1) % F)

    loads = [pltpu.make_async_copy(src, dst, lsem.at[n]) for n, (src, dst) in enumerate(
        [(video, vloc), (na, ga), (ca, ka), (nb, gb), (cb, kb), (nc, gc),
         (wq, sq), (wk, sk), (wv, sv), (wo, so)])]
    for load in loads:
        load.start()

    barrier = pltpu.get_barrier_semaphore()

    def greet(k, carry):
        pl.semaphore_signal(barrier, inc=1, device_id=((f + k) % F, r), device_id_type=MESH)
        return carry

    lax.fori_loop(1, F, greet, 0)
    for rr in (up, down):
        for ff in (west, f, east):
            pl.semaphore_signal(barrier, inc=1, device_id=(ff, rr), device_id_type=MESH)

    fwd[...] = one_hot(lambda a: (a % T) * 16 + a // T)
    bwd[...] = one_hot(lambda a: (a % 16) * T + a // 16)
    pl.semaphore_wait(barrier, F - 1 + 6)
    loads[0].wait()

    def in_copy(k):
        peer = (f + k) % F
        return pltpu.make_async_remote_copy(
            vloc.at[:, :, snake(peer)], rin.at[f], in_send.at[k], in_recv.at[f],
            device_id=(peer, r), device_id_type=MESH)

    def in_start(k, carry):
        in_copy(k).start()
        return carry

    lax.fori_loop(1, F, in_start, 0)
    rin[f] = vloc[:, :, g]

    def in_wait(k, carry):
        src = (f + k) % F
        pltpu.make_async_remote_copy(
            vloc.at[:, :, snake(src)], rin.at[src], in_send.at[k], in_recv.at[src],
            device_id=(src, r), device_id_type=MESH).wait()
        return carry

    lax.fori_loop(1, F, in_wait, 0)

    loads[1].wait()
    x = dot(fwd[...], rin[...].reshape(512, C))
    xres[...] = x.astype(BF).reshape(2, PATCH, T, C)
    act_a[1:3, 1 : PATCH + 1] = silu(rms(x, ga[...])).astype(BF).reshape(2, PATCH, T, C)

    def halo(buf, send, recv):
        mid = pl.ds(1, PATCH)
        plan = [
            (buf.at[1, mid], buf.at[3, mid], (f, up)),
            (buf.at[2, mid], buf.at[0, mid], (f, down)),
            (buf.at[pl.ds(1, 2), 1], buf.at[pl.ds(1, 2), PATCH + 1], (west, r)),
            (buf.at[pl.ds(1, 2), PATCH], buf.at[pl.ds(1, 2), 0], (east, r)),
            (buf.at[1, 1], buf.at[3, PATCH + 1], (west, up)),
            (buf.at[1, PATCH], buf.at[3, 0], (east, up)),
            (buf.at[2, 1], buf.at[0, PATCH + 1], (west, down)),
            (buf.at[2, PATCH], buf.at[0, 0], (east, down)),
        ]
        copies = [
            pltpu.make_async_remote_copy(
                src, dst, send.at[n], recv.at[n], device_id=to, device_id_type=MESH)
            for n, (src, dst, to) in enumerate(plan)
        ]
        for copy in copies:
            copy.start()
        return copies

    def halo_end(buf, copies):
        for copy in copies:
            copy.wait()

        @pl.when(r == 0)
        def _():
            buf[0] = jnp.zeros((PATCH + 2, T, C), BF)

        @pl.when(r == R - 1)
        def _():
            buf[3] = jnp.zeros((PATCH + 2, T, C), BF)

        @pl.when(g == 0)
        def _():
            buf[:, 0] = jnp.zeros((4, T, C), BF)

        @pl.when(g == F - 1)
        def _():
            buf[:, PATCH + 1] = jnp.zeros((4, T, C), BF)

    copies = halo(act_a, ha_send, ha_recv)
    for load in loads[2:]:
        load.wait()
    halo_end(act_a, copies)

    def conv_one(row, carry):
        inner = conv_rows(act_a, ka, row).astype(BF).astype(F32)
        act = silu(rms(inner, gb[...])).astype(BF)
        act_b[row + 1, 1 : PATCH + 1] = act.reshape(PATCH, T, C)
        return carry

    lax.fori_loop(0, 2, conv_one, 0)
    copies = halo(act_b, hb_send, hb_recv)
    halo_end(act_b, copies)

    def conv_two(row, carry):
        res = xres[row].reshape(PATCH * T, C).astype(F32)
        block = (res + conv_rows(act_b, kb, row)).astype(BF)
        blk[row] = block.reshape(PATCH, T, C)
        normed = rms(block.astype(F32), gc[...]).astype(BF)
        for w, dst in ((sq, qs), (sk, ks), (sv, vs)):
            dst[pl.ds(row * PATCH, PATCH)] = dot(normed, w[...]).astype(BF).reshape(PATCH, T, C)
        return carry

    lax.fori_loop(0, 2, conv_two, 0)

    def attend(p, carry):
        for n in range(2):
            at = 2 * p + n
            low, high = attend_pixel(qs[at], ks[at], vs[at])
            att[at, :, 0:128] = low
            att[at, :, 128:256] = high
        return carry

    lax.fori_loop(0, 8, attend, 0)

    projected = dot(att[...].reshape(512, C), so[...]).astype(BF).astype(F32)
    encoded = (blk[...].reshape(512, C).astype(F32) + projected).astype(BF)
    sbuf[...] = dot(bwd[...], encoded).astype(BF).reshape(F, 2, 2, PATCH, C)

    def out_start(k, carry):
        peer = (f + k) % F
        pltpu.make_async_remote_copy(
            sbuf.at[peer], out.at[:, :, g], out_send.at[k], out_recv.at[f],
            device_id=(peer, r), device_id_type=MESH).start()
        return carry

    lax.fori_loop(1, F, out_start, 0)
    own = pltpu.make_async_copy(sbuf.at[f], out.at[:, :, g], lsem.at[0])
    own.start()

    def out_wait(k, carry):
        src = (f + k) % F
        pltpu.make_async_remote_copy(
            sbuf.at[src], out.at[:, :, snake(src)], out_send.at[k], out_recv.at[src],
            device_id=(src, r), device_id_type=MESH).wait()
        return carry

    lax.fori_loop(1, F, out_wait, 0)
    own.wait()


def shards(video, na, ca, nb, cb, nc, wq, wk, wv, wo):
    any_spec = pl.BlockSpec(memory_space=pl.ANY)
    dma = pltpu.SemaphoreType.DMA
    vm = pltpu.VMEM
    pix = (2 * PATCH, T, C)
    halo = (4, PATCH + 2, T, C)
    out = pl.pallas_call(
        kernel,
        out_shape=jax.ShapeDtypeStruct((2, 2, F, PATCH, C), BF),
        in_specs=[any_spec] * 10,
        out_specs=any_spec,
        scratch_shapes=[
            vm((2, 2, F, PATCH, C), BF), vm((F, 2, 2, PATCH, C), BF), vm((2, PATCH, T, C), BF),
            vm(halo, BF), vm(halo, BF), vm((27, C, C), BF), vm((27, C, C), BF),
            vm((1, C), F32), vm((1, C), F32), vm((1, C), F32),
            vm((C, C), BF), vm((C, C), BF), vm((C, C), BF), vm((C, C), BF),
            vm((512, 512), BF), vm((512, 512), BF),
            vm(pix, BF), vm(pix, BF), vm(pix, BF), vm(pix, BF), vm((2, PATCH, T, C), BF),
            vm((F, 2, 2, PATCH, C), BF),
            dma((10,)), dma((F,)), dma((F,)), dma((8,)), dma((8,)), dma((8,)), dma((8,)),
            dma((F,)), dma((F,)),
        ],
        compiler_params=pltpu.CompilerParams(
            collective_id=0, has_side_effects=True, vmem_limit_bytes=60 * 1024 * 1024),
    )(
        video.reshape(2, 2, F, PATCH, C), na.reshape(1, C), ca.reshape(27, C, C), nb.reshape(1, C),
        cb.reshape(27, C, C), nc.reshape(1, C), wq, wk, wv, wo,
    )
    return out.reshape(2, 2, F * PATCH, C)


def solution(mesh):
    placed = (P("frames", "rows", None, None), P(), P(), P(), P(), P(), P(), P(), P(), P())
    return jax.shard_map(
        shards,
        mesh=mesh,
        in_specs=placed,
        out_specs=P("frames", "rows", None, None),
        check_vma=False,
    )
```

time: 116 us -> 55.2 us (0.48)
  the two profiles are of different devices: /device:TPU:8 before, /device:TPU:4 now
where the time goes in v1:
time: 55.2 us; the launch traced here: 54.7 us
  Pallas kernels  53.1 us (96%)
  local copies, waits for them, and re-layouts  1.67 us (3%)
    pallas_call x1, Pallas kernels, shards(): pl.pallas_call(kernel, out_shape=jax.ShapeDtypeStruct((2, 2, F, PATCH, C)...  53.1 us
    unnamed x1, local copies, waits for them, and re-layouts  1.67 us

profile of v1, /device:TPU:4, one launch (start us, length us, event | category | flops | bytes accessed | tf_op | source)
XLA Modules:
  0.0 54.7 jit_solution(2560371771739250979)
XLA Ops:
  0.0 53.1 %shard_map.100 = bf16[2,2,16,8,256]{4,3,2,1,0:T(8,128)(2,1)} custom-call(bf16[2,2,16,8,256]{4,3,2,1,0:T(8,128)(2,1)} %bitcast.10, f32[1,256]{1,0:T(1,128)} %bitcast.11, bf16[27,256,256]{2,1,0:T(8,128)(2,1)} %bitcast.7, f32[1,256]{1,0:T(1,128)} %bitcast.12, bf16[27,256,256]{2,1,0:T(8,128)(2,1)} %bitcast.8, f32[1,256]{1,0:T(1,128)} %bitcast.13, ...), custom_call_target="tpu_custom_call" | custom-call | tf_op jit(solution)/shard_map/pallas_call | solution.py:259
  53.1 1.7 %copy.12 = bf16[2,2,128,256]{3,2,1,0:T(8,128)(2,1)} copy(bf16[2,2,128,256]{3,2,1,0:T(8,128)(2,1)} %bitcast.9) | data formatting | bytes 524288

commit v2 on v1

v2 whole, which is shorter than its diff:
```python
import functools

import jax
import jax.numpy as jnp
from jax import lax
from jax.experimental import pallas as pl
from jax.experimental.pallas import tpu as pltpu
from jax.sharding import PartitionSpec as P

MESH = pl.DeviceIdType.MESH
HEADS = 8
C = 256
T = 32
H = 16
F = 16
R = 16
PATCH = 8
BF = jnp.bfloat16
F32 = jnp.float32


def snake(i):
    half = i // 8
    return i + half * (23 - 2 * i)


def rms(x, gain):
    ms = jnp.mean(x * x, axis=-1, keepdims=True)
    return x * lax.rsqrt(ms + 1e-06) * gain


def silu(x):
    h = 0.5 * x
    return h + h * jnp.tanh(h)


def dot(a, b):
    return jnp.dot(a, b, preferred_element_type=F32)


def dot_tt(a, b, dims):
    return lax.dot_general(a, b, (dims, ((), ())), preferred_element_type=F32)


def conv_half(act, kern, y1, y0, h):
    slabs = [
        act[h, j : j + 2, l : l + PATCH].reshape(256, C) for j in range(3) for l in range(3)
    ]
    parts = []
    for i in range(3):
        total = dot(slabs[0], kern[i * 9])
        for n in range(1, 9):
            total = total + dot(slabs[n], kern[i * 9 + n])
        parts.append(total)
    at = 8 + H * h
    y1[:, at : at + H] = parts[1].reshape(16, H, C)
    y0[:, at : at + H] = parts[0].reshape(16, H, C)
    late = y1[:, at - 1 : at - 1 + H] + y0[:, at - 2 : at - 2 + H]
    return parts[2] + late.reshape(256, C)


def iota(shape, dim):
    return lax.broadcasted_iota(jnp.int32, shape, dim)


def attend_half(h, qs, ks, vs, att, hmask):
    keys = H * (h + 1)
    group = 128 // keys
    scale = 32 ** -0.5
    causal = iota((1, keys, 128), 1) <= (iota((1, keys, 128), 2) & 15) + H * h
    lane_head = iota((H, 128), 1) >> 5
    row_pixel = iota((128, 128), 0) >> (4 + h)
    for u in range(16 // group):
        pixels = range(u * group, (u + 1) * group)
        scores = []
        for p in pixels:
            q_bd = jnp.concatenate([qs[h, p]] * 8, axis=0) * hmask[...]
            scores.append(dot_tt(ks[p, 0:keys], q_bd, ((1,), (1,))))
        s = jnp.concatenate(scores, axis=0).reshape(group, keys, 128)
        s = jnp.where(causal, s, -1e30)
        e = jnp.exp((s - jnp.max(s, axis=1, keepdims=True)) * scale)
        probs = (e * (1.0 / jnp.sum(e, axis=1, keepdims=True))).astype(BF)
        probs = probs.reshape(128, 128).T
        value = vs[pl.ds(u * group, group), 0:keys].reshape(128, C)
        for hh in range(2):
            lanes = slice(128 * hh, 128 * hh + 128)
            part = value[:, lanes]
            v_bd = jnp.concatenate(
                [part * (row_pixel == n).astype(BF) for n in range(group)], axis=1)
            o = dot(probs[64 * hh : 64 * hh + 64], v_bd)
            for n, p in enumerate(pixels):
                tile = o[:, 128 * n : 128 * n + 128]
                got = tile[0:16]
                for k in range(1, 4):
                    got = jnp.where(lane_head == k, tile[16 * k : 16 * k + 16], got)
                att[p, :, lanes] = got.astype(BF)


def kernel(video, na, ca, nb, cb, nc, wq, wk, wv, wo, out,
           vloc, rin, xres, act_a, act_b, ka, kb, ga, gb, gc, sq, sk, sv, so,
           perm, hmask, y1, y0, qs, ks, vs, att, blk, sbuf,
           lsem, in_send, in_recv, ha_send, ha_recv, hb_send, hb_recv, out_send, out_recv):
    f = lax.axis_index("frames")
    r = lax.axis_index("rows")
    g = snake(f)
    mine = f // 8
    up, down = (r + R - 1) % R, (r + 1) % R
    west, east = snake((g + F - 1) % F), snake((g + 1) % F)

    loads = [pltpu.make_async_copy(src, dst, lsem.at[n]) for n, (src, dst) in enumerate(
        [(video, vloc), (na, ga), (ca, ka), (nb, gb), (cb, kb), (nc, gc),
         (wq, sq), (wk, sk), (wv, sv), (wo, so)])]
    for load in loads:
        load.start()

    barrier = pltpu.get_barrier_semaphore()

    def greet(k, carry):
        pl.semaphore_signal(barrier, inc=1, device_id=((f + k) % F, r), device_id_type=MESH)
        return carry

    lax.fori_loop(1, F, greet, 0)
    for rr in (up, down):
        for ff in (west, f, east):
            pl.semaphore_signal(barrier, inc=1, device_id=(ff, rr), device_id_type=MESH)

    a, b = iota((256, 256), 0), iota((256, 256), 1)
    perm[...] = jnp.where(b == ((a & 15) << 4) + (a >> 4), 1.0, 0.0).astype(BF)
    hmask[...] = jnp.where(
        (iota((128, C), 0) >> 4) == (iota((128, C), 1) >> 5), 1.0, 0.0).astype(BF)
    y1[:, 0:8] = jnp.zeros((16, 8, C), F32)
    y0[:, 0:8] = jnp.zeros((16, 8, C), F32)
    pl.semaphore_wait(barrier, F - 1 + 6)
    loads[0].wait()

    def in_copy(k, peer, source):
        return pltpu.make_async_remote_copy(
            vloc.at[:, :, snake(peer)], rin.at[source], in_send.at[k], in_recv.at[source],
            device_id=(peer, r), device_id_type=MESH)

    def in_start(k, carry):
        in_copy(k, (f + k) % F, f).start()
        return carry

    lax.fori_loop(1, F, in_start, 0)
    rin[f] = vloc[:, :, g]
    for load in loads[1:]:
        load.wait()


    def halo(buf, send, recv, h):
        b = buf.at[h]
        mid = pl.ds(1, PATCH)
        plan = [
            (b.at[1, mid], b.at[3, mid], (f, up)),
            (b.at[2, mid], b.at[0, mid], (f, down)),
            (b.at[pl.ds(1, 2), 1], b.at[pl.ds(1, 2), PATCH + 1], (west, r)),
            (b.at[pl.ds(1, 2), PATCH], b.at[pl.ds(1, 2), 0], (east, r)),
            (b.at[1, 1], b.at[3, PATCH + 1], (west, up)),
            (b.at[1, PATCH], b.at[3, 0], (east, up)),
            (b.at[2, 1], b.at[0, PATCH + 1], (west, down)),
            (b.at[2, PATCH], b.at[0, 0], (east, down)),
        ]
        copies = [
            pltpu.make_async_remote_copy(
                src, dst, send.at[8 * h + n], recv.at[8 * h + n],
                device_id=to, device_id_type=MESH)
            for n, (src, dst, to) in enumerate(plan)
        ]
        for copy in copies:
            copy.start()
        return copies

    def halo_end(buf, copies, h):
        for copy in copies:
            copy.wait()

        @pl.when(r == 0)
        def _():
            buf[h, 0] = jnp.zeros((PATCH + 2, H, C), BF)

        @pl.when(r == R - 1)
        def _():
            buf[h, 3] = jnp.zeros((PATCH + 2, H, C), BF)

        @pl.when(g == 0)
        def _():
            buf[h, :, 0] = jnp.zeros((4, H, C), BF)

        @pl.when(g == F - 1)
        def _():
            buf[h, :, PATCH + 1] = jnp.zeros((4, H, C), BF)

    halos_a, halos_b = [], []
    for h in range(2):
        def in_wait(k, carry):
            src = 8 * h + k

            @pl.when(src != f)
            def _():
                in_copy(0, src, src).wait_recv()
            return carry

        lax.fori_loop(0, 8, in_wait, 0)
        x = dot(perm[...], rin[8 * h : 8 * h + 8].reshape(256, C))
        xres[h] = x.astype(BF)
        act = silu(rms(x, ga[...])).astype(BF)
        act_a[h, 1:3, 1 : PATCH + 1] = act.reshape(2, PATCH, H, C)
        halos_a.append(halo(act_a, ha_send, ha_recv, h))

    for h in range(2):
        halo_end(act_a, halos_a[h], h)
        inner = conv_half(act_a, ka, y1, y0, h).astype(BF).astype(F32)
        act = silu(rms(inner, gb[...])).astype(BF)
        act_b[h, 1:3, 1 : PATCH + 1] = act.reshape(2, PATCH, H, C)
        halos_b.append(halo(act_b, hb_send, hb_recv, h))

    def out_copy(dst, source, k):
        return pltpu.make_async_remote_copy(
            sbuf.at[dst], out.at[:, :, snake(source)], out_send.at[k], out_recv.at[source],
            device_id=(dst, r), device_id_type=MESH)

    own = pltpu.make_async_copy(sbuf.at[f], out.at[:, :, g], lsem.at[0])
    for h in range(2):
        halo_end(act_b, halos_b[h], h)
        block = (xres[h].astype(F32) + conv_half(act_b, kb, y1, y0, h)).astype(BF)
        blk[...] = block
        normed = rms(block.astype(F32), gc[...]).astype(BF)
        qs[h] = dot(normed, sq[...]).astype(BF).reshape(16, H, C)
        ks[:, H * h : H * h + H] = dot(normed, sk[...]).astype(BF).reshape(16, H, C)
        vs[:, H * h : H * h + H] = dot(normed, sv[...]).astype(BF).reshape(16, H, C)
        attend_half(h, qs, ks, vs, att, hmask)
        projected = dot(att[...].reshape(256, C), so[...]).astype(BF).astype(F32)
        encoded = (blk[...].astype(F32) + projected).astype(BF)
        sbuf[8 * h : 8 * h + 8] = dot(perm[...], encoded).astype(BF).reshape(8, 2, 2, PATCH, C)

        @pl.when(mine == h)
        def _():
            own.start()

        @pl.when(mine != h)
        def _():
            out_copy(8 * h + f % 8, f, 8 * h).start()

        def out_start(k, carry):
            out_copy(8 * h + (f + k) % 8, f, 8 * h + k).start()
            return carry

        lax.fori_loop(1, 8, out_start, 0)

    def finish(k, carry):
        src = (f + k) % F
        in_copy(k, src, src).wait_send()
        out_copy(src, src, k).wait_recv()
        return carry

    lax.fori_loop(1, F, finish, 0)
    own.wait()

    def sent(k, carry):
        @pl.when(k != 8 * mine)
        def _():
            out_copy((f + 1) % F, f, k).wait_send()
        return carry

    lax.fori_loop(0, F, sent, 0)


def shards(video, na, ca, nb, cb, nc, wq, wk, wv, wo):
    any_spec = pl.BlockSpec(memory_space=pl.ANY)
    dma = pltpu.SemaphoreType.DMA
    vm = pltpu.VMEM
    halo = (2, 4, PATCH + 2, H, C)
    out = pl.pallas_call(
        kernel,
        out_shape=jax.ShapeDtypeStruct((2, 2, F, PATCH, C), BF),
        in_specs=[any_spec] * 10,
        out_specs=any_spec,
        scratch_shapes=[
            vm((2, 2, F, PATCH, C), BF), vm((F, 2, 2, PATCH, C), BF), vm((2, 256, C), BF),
            vm(halo, BF), vm(halo, BF), vm((27, C, C), BF), vm((27, C, C), BF),
            vm((1, C), F32), vm((1, C), F32), vm((1, C), F32),
            vm((C, C), BF), vm((C, C), BF), vm((C, C), BF), vm((C, C), BF),
            vm((256, 256), BF), vm((128, C), BF), vm((16, 40, C), F32), vm((16, 40, C), F32),
            vm((2, 16, H, C), BF), vm((16, T, C), BF), vm((16, T, C), BF), vm((16, H, C), BF),
            vm((256, C), BF), vm((F, 2, 2, PATCH, C), BF),
            dma((10,)), dma((F,)), dma((F,)), dma((16,)), dma((16,)), dma((16,)), dma((16,)),
            dma((F,)), dma((F,)),
        ],
        compiler_params=pltpu.CompilerParams(
            collective_id=0, has_side_effects=True, vmem_limit_bytes=60 * 1024 * 1024),
    )(
        video.reshape(2, 2, F, PATCH, C), na.reshape(1, C), ca.reshape(27, C, C), nb.reshape(1, C),
        cb.reshape(27, C, C), nc.reshape(1, C), wq, wk, wv, wo,
    )
    return out.reshape(2, 2, F * PATCH, C)


def solution(mesh):
    placed = (P("frames", "rows", None, None), P(), P(), P(), P(), P(), P(), P(), P(), P())
    return jax.shard_map(
        shards,
        mesh=mesh,
        in_specs=placed,
        out_specs=P("frames", "rows", None, None),
        check_vma=False,
    )
```

time: 55.2 us -> 44.8 us (0.81)
  Pallas kernels: 53.1 us -> 43 us
    pallas_call x1, Pallas kernels: 53.1 us -> 43 us  [shards(): pl.pallas_call(kernel, out_shape=jax.ShapeDtypeStruct((2, 2, F, PATCH, C)...]
where the time goes in v2:
time: 44.8 us; the launch traced here: 44.7 us
  Pallas kernels  43 us (96%)
  local copies, waits for them, and re-layouts  1.67 us (4%)
    pallas_call x1, Pallas kernels, shards(): pl.pallas_call(kernel, out_shape=jax.ShapeDtypeStruct((2, 2, F, PATCH, C)...  43 us
    unnamed x1, local copies, waits for them, and re-layouts  1.67 us

profile of v2, /device:TPU:4, one launch (start us, length us, event | category | flops | bytes accessed | tf_op | source)
XLA Modules:
  0.0 44.7 jit_solution(6172357495050134946)
XLA Ops:
  0.0 43.0 %shard_map.100 = bf16[2,2,16,8,256]{4,3,2,1,0:T(8,128)(2,1)} custom-call(bf16[2,2,16,8,256]{4,3,2,1,0:T(8,128)(2,1)} %bitcast.10, f32[1,256]{1,0:T(1,128)} %bitcast.11, bf16[27,256,256]{2,1,0:T(8,128)(2,1)} %bitcast.7, f32[1,256]{1,0:T(1,128)} %bitcast.12, bf16[27,256,256]{2,1,0:T(8,128)(2,1)} %bitcast.8, f32[1,256]{1,0:T(1,128)} %bitcast.13, ...), custom_call_target="tpu_custom_call" | custom-call | tf_op jit(solution)/shard_map/pallas_call | solution.py:274
  43.0 1.7 %copy.12 = bf16[2,2,128,256]{3,2,1,0:T(8,128)(2,1)} copy(bf16[2,2,128,256]{3,2,1,0:T(8,128)(2,1)} %bitcast.9) | data formatting | bytes 524288

commit v3 on v2

--- a/solution.py
+++ b/solution.py
@@ -42,35 +42,55 @@
     return lax.dot_general(a, b, (dims, ((), ())), preferred_element_type=F32)
 
 
-def conv_half(act, kern, y1, y0, h):
+def inner_taps(act, kern, ys, h):
     slabs = [
         act[h, j : j + 2, l : l + PATCH].reshape(256, C) for j in range(3) for l in range(3)
     ]
-    parts = []
+    at = 8 + H * h
     for i in range(3):
         total = dot(slabs[0], kern[i * 9])
         for n in range(1, 9):
             total = total + dot(slabs[n], kern[i * 9 + n])
-        parts.append(total)
+        ys[i, :, at : at + H] = total.reshape(16, H, C)
+
+
+def edge_taps(north, south, west, east, kern, ys, h):
+    rows = slice(8 + H * h, 8 + H * h + H)
+
+    def chain(terms):
+        total = None
+        for lhs, tap in terms:
+            term = dot(lhs.reshape(-1, C), kern[tap])
+            total = term if total is None else total + term
+        return total
+
+    for i in range(3):
+        top = chain([(north[h, l : l + PATCH], i * 9 + l) for l in range(3)])
+        low = chain([(south[h, l : l + PATCH], i * 9 + 6 + l) for l in range(3)])
+        left = chain([(west[h, j : j + 2], i * 9 + 3 * j) for j in range(3)])
+        right = chain([(east[h, j : j + 2], i * 9 + 3 * j + 2) for j in range(3)])
+        ys[i, 0:8, rows] += top.reshape(8, H, C)
+        ys[i, 8:16, rows] += low.reshape(8, H, C)
+        for row in range(2):
+            ys[i, 8 * row, rows] += left[H * row : H * row + H]
+            ys[i, 8 * row + 7, rows] += right[H * row : H * row + H]
     at = 8 + H * h
-    y1[:, at : at + H] = parts[1].reshape(16, H, C)
-    y0[:, at : at + H] = parts[0].reshape(16, H, C)
-    late = y1[:, at - 1 : at - 1 + H] + y0[:, at - 2 : at - 2 + H]
-    return parts[2] + late.reshape(256, C)
+    total = ys[2, :, at : at + H] + ys[1, :, at - 1 : at - 1 + H] + ys[0, :, at - 2 : at - 2 + H]
+    return total.reshape(256, C)
 
 
 def iota(shape, dim):
     return lax.broadcasted_iota(jnp.int32, shape, dim)
 
 
-def attend_half(h, qs, ks, vs, att, hmask):
+def attend_row(h, row, qs, ks, vs, att, hmask):
     keys = H * (h + 1)
     group = 128 // keys
     scale = 32 ** -0.5
     causal = iota((1, keys, 128), 1) <= (iota((1, keys, 128), 2) & 15) + H * h
     lane_head = iota((H, 128), 1) >> 5
     row_pixel = iota((128, 128), 0) >> (4 + h)
-    for u in range(16 // group):
+    for u in range(row * 8 // group, (row + 1) * 8 // group):
         pixels = range(u * group, (u + 1) * group)
         scores = []
         for p in pixels:
@@ -98,7 +118,7 @@
 
 def kernel(video, na, ca, nb, cb, nc, wq, wk, wv, wo, out,
            vloc, rin, xres, act_a, act_b, ka, kb, ga, gb, gc, sq, sk, sv, so,
-           perm, hmask, y1, y0, qs, ks, vs, att, blk, sbuf,
+           perm, perm_row, hmask, ya, yb, na_h, sa_h, wa_h, ea_h, nb_h, sb_h, wb_h, eb_h, qs, ks, vs, att, blk, sbuf,
            lsem, in_send, in_recv, ha_send, ha_recv, hb_send, hb_recv, out_send, out_recv):
     f = lax.axis_index("frames")
     r = lax.axis_index("rows")
@@ -128,8 +148,18 @@
     perm[...] = jnp.where(b == ((a & 15) << 4) + (a >> 4), 1.0, 0.0).astype(BF)
     hmask[...] = jnp.where(
         (iota((128, C), 0) >> 4) == (iota((128, C), 1) >> 5), 1.0, 0.0).astype(BF)
-    y1[:, 0:8] = jnp.zeros((16, 8, C), F32)
-    y0[:, 0:8] = jnp.zeros((16, 8, C), F32)
+    a, b = iota((128, 128), 0), iota((128, 128), 1)
+    perm_row[...] = jnp.where(b == ((a & 7) << 4) + (a >> 3), 1.0, 0.0).astype(BF)
+    for ys in (ya, yb):
+        ys[:, :, 0:8] = jnp.zeros((3, 16, 8, C), F32)
+    for buf in (act_a, act_b):
+        for at in (0, 3):
+            buf[:, at] = jnp.zeros((2, PATCH + 2, H, C), BF)
+        for at in (0, PATCH + 1):
+            buf[:, 1:3, at] = jnp.zeros((2, 2, H, C), BF)
+    for buf in (wa_h, ea_h, wb_h, eb_h):
+        for at in (0, 3):
+            buf[:, at] = jnp.zeros((2, H, C), BF)
     pl.semaphore_wait(barrier, F - 1 + 6)
     loads[0].wait()
 
@@ -148,18 +178,19 @@
         load.wait()
 
 
-    def halo(buf, send, recv, h):
+    def halo(buf, lands, send, recv, h):
         b = buf.at[h]
-        mid = pl.ds(1, PATCH)
+        north, south, west_h, east_h = (land.at[h] for land in lands)
+        mid, two = pl.ds(1, PATCH), pl.ds(1, 2)
         plan = [
-            (b.at[1, mid], b.at[3, mid], (f, up)),
-            (b.at[2, mid], b.at[0, mid], (f, down)),
-            (b.at[pl.ds(1, 2), 1], b.at[pl.ds(1, 2), PATCH + 1], (west, r)),
-            (b.at[pl.ds(1, 2), PATCH], b.at[pl.ds(1, 2), 0], (east, r)),
-            (b.at[1, 1], b.at[3, PATCH + 1], (west, up)),
-            (b.at[1, PATCH], b.at[3, 0], (east, up)),
-            (b.at[2, 1], b.at[0, PATCH + 1], (west, down)),
-            (b.at[2, PATCH], b.at[0, 0], (east, down)),
+            (b.at[1, mid], south.at[mid], (f, up)),
+            (b.at[2, mid], north.at[mid], (f, down)),
+            (b.at[1, 1], south.at[PATCH + 1], (west, up)),
+            (b.at[1, PATCH], south.at[0], (east, up)),
+            (b.at[2, 1], north.at[PATCH + 1], (west, down)),
+            (b.at[2, PATCH], north.at[0], (east, down)),
+            (b.at[two, 1], east_h.at[two], (west, r)),
+            (b.at[two, PATCH], west_h.at[two], (east, r)),
         ]
         copies = [
             pltpu.make_async_remote_copy(
@@ -171,26 +202,33 @@
             copy.start()
         return copies
 
-    def halo_end(buf, copies, h):
+    def halo_end(lands, copies, h):
         for copy in copies:
             copy.wait()
+        north, south, west_h, east_h = lands
 
         @pl.when(r == 0)
         def _():
-            buf[h, 0] = jnp.zeros((PATCH + 2, H, C), BF)
+            north[h] = jnp.zeros((PATCH + 2, H, C), BF)
 
         @pl.when(r == R - 1)
         def _():
-            buf[h, 3] = jnp.zeros((PATCH + 2, H, C), BF)
+            south[h] = jnp.zeros((PATCH + 2, H, C), BF)
 
         @pl.when(g == 0)
         def _():
-            buf[h, :, 0] = jnp.zeros((4, H, C), BF)
+            north[h, 0] = jnp.zeros((H, C), BF)
+            south[h, 0] = jnp.zeros((H, C), BF)
+            west_h[h, 1:3] = jnp.zeros((2, H, C), BF)
 
         @pl.when(g == F - 1)
         def _():
-            buf[h, :, PATCH + 1] = jnp.zeros((4, H, C), BF)
-
+            north[h, PATCH + 1] = jnp.zeros((H, C), BF)
+            south[h, PATCH + 1] = jnp.zeros((H, C), BF)
+            east_h[h, 1:3] = jnp.zeros((2, H, C), BF)
+
+    lands_a = (na_h, sa_h, wa_h, ea_h)
+    lands_b = (nb_h, sb_h, wb_h, eb_h)
     halos_a, halos_b = [], []
     for h in range(2):
         def in_wait(k, carry):
@@ -206,64 +244,67 @@
         xres[h] = x.astype(BF)
         act = silu(rms(x, ga[...])).astype(BF)
         act_a[h, 1:3, 1 : PATCH + 1] = act.reshape(2, PATCH, H, C)
-        halos_a.append(halo(act_a, ha_send, ha_recv, h))
-
-    for h in range(2):
-        halo_end(act_a, halos_a[h], h)
-        inner = conv_half(act_a, ka, y1, y0, h).astype(BF).astype(F32)
+        halos_a.append(halo(act_a, lands_a, ha_send, ha_recv, h))
+
+    for h in range(2):
+        inner_taps(act_a, ka, ya, h)
+    for h in range(2):
+        halo_end(lands_a, halos_a[h], h)
+        inner = edge_taps(*lands_a, ka, ya, h).astype(BF).astype(F32)
         act = silu(rms(inner, gb[...])).astype(BF)
         act_b[h, 1:3, 1 : PATCH + 1] = act.reshape(2, PATCH, H, C)
-        halos_b.append(halo(act_b, hb_send, hb_recv, h))
-
-    def out_copy(dst, source, k):
+        halos_b.append(halo(act_b, lands_b, hb_send, hb_recv, h))
+    for h in range(2):
+        inner_taps(act_b, kb, yb, h)
+
+    def out_copy(dst, source, row, k):
         return pltpu.make_async_remote_copy(
-            sbuf.at[dst], out.at[:, :, snake(source)], out_send.at[k], out_recv.at[source],
+            sbuf.at[dst, row], out.at[:, row, snake(source)],
+            out_send.at[2 * k + row], out_recv.at[2 * source + row],
             device_id=(dst, r), device_id_type=MESH)
 
-    own = pltpu.make_async_copy(sbuf.at[f], out.at[:, :, g], lsem.at[0])
-    for h in range(2):
-        halo_end(act_b, halos_b[h], h)
-        block = (xres[h].astype(F32) + conv_half(act_b, kb, y1, y0, h)).astype(BF)
+    own = [pltpu.make_async_copy(sbuf.at[f, row], out.at[:, row, g], lsem.at[row])
+           for row in range(2)]
+    for h in range(2):
+        halo_end(lands_b, halos_b[h], h)
+        block = (xres[h].astype(F32) + edge_taps(*lands_b, kb, yb, h)).astype(BF)
         blk[...] = block
         normed = rms(block.astype(F32), gc[...]).astype(BF)
         qs[h] = dot(normed, sq[...]).astype(BF).reshape(16, H, C)
         ks[:, H * h : H * h + H] = dot(normed, sk[...]).astype(BF).reshape(16, H, C)
         vs[:, H * h : H * h + H] = dot(normed, sv[...]).astype(BF).reshape(16, H, C)
-        attend_half(h, qs, ks, vs, att, hmask)
-        projected = dot(att[...].reshape(256, C), so[...]).astype(BF).astype(F32)
-        encoded = (blk[...].astype(F32) + projected).astype(BF)
-        sbuf[8 * h : 8 * h + 8] = dot(perm[...], encoded).astype(BF).reshape(8, 2, 2, PATCH, C)
-
-        @pl.when(mine == h)
-        def _():
-            own.start()
-
-        @pl.when(mine != h)
-        def _():
-            out_copy(8 * h + f % 8, f, 8 * h).start()
-
-        def out_start(k, carry):
-            out_copy(8 * h + (f + k) % 8, f, 8 * h + k).start()
-            return carry
-
-        lax.fori_loop(1, 8, out_start, 0)
+        for row in range(2):
+            attend_row(h, row, qs, ks, vs, att, hmask)
+            at = slice(128 * row, 128 * row + 128)
+            projected = dot(att[8 * row : 8 * row + 8].reshape(128, C), so[...])
+            encoded = (blk[at].astype(F32) + projected.astype(BF).astype(F32)).astype(BF)
+            moved = dot(perm_row[...], encoded).astype(BF)
+            sbuf[8 * h : 8 * h + 8, row] = moved.reshape(8, 2, PATCH, C)
+
+            @pl.when(mine == h)
+            def _():
+                own[row].start()
+
+            def out_start(k, carry):
+                dst = 8 * h + k
+
+                @pl.when(dst != f)
+                def _():
+                    out_copy(dst, f, row, dst).start()
+                return carry
+
+            lax.fori_loop(0, 8, out_start, 0)
 
     def finish(k, carry):
         src = (f + k) % F
         in_copy(k, src, src).wait_send()
-        out_copy(src, src, k).wait_recv()
+        for row in range(2):
+            out_copy(src, src, row, src).wait()
         return carry
 
     lax.fori_loop(1, F, finish, 0)
-    own.wait()
-
-    def sent(k, carry):
-        @pl.when(k != 8 * mine)
-        def _():
-            out_copy((f + 1) % F, f, k).wait_send()
-        return carry
-
-    lax.fori_loop(0, F, sent, 0)
+    for copy in own:
+        copy.wait()
 
 
 def shards(video, na, ca, nb, cb, nc, wq, wk, wv, wo):
@@ -271,6 +312,7 @@
     dma = pltpu.SemaphoreType.DMA
     vm = pltpu.VMEM
     halo = (2, 4, PATCH + 2, H, C)
+    lands = [vm((2, n, H, C), BF) for n in (PATCH + 2, PATCH + 2, 4, 4)]
     out = pl.pallas_call(
         kernel,
         out_shape=jax.ShapeDtypeStruct((2, 2, F, PATCH, C), BF),
@@ -281,11 +323,13 @@
             vm(halo, BF), vm(halo, BF), vm((27, C, C), BF), vm((27, C, C), BF),
             vm((1, C), F32), vm((1, C), F32), vm((1, C), F32),
             vm((C, C), BF), vm((C, C), BF), vm((C, C), BF), vm((C, C), BF),
-            vm((256, 256), BF), vm((128, C), BF), vm((16, 40, C), F32), vm((16, 40, C), F32),
+            vm((256, 256), BF), vm((128, 128), BF), vm((128, C), BF),
+            vm((3, 16, 40, C), F32), vm((3, 16, 40, C), F32),
+            *lands, *lands,
             vm((2, 16, H, C), BF), vm((16, T, C), BF), vm((16, T, C), BF), vm((16, H, C), BF),
             vm((256, C), BF), vm((F, 2, 2, PATCH, C), BF),
             dma((10,)), dma((F,)), dma((F,)), dma((16,)), dma((16,)), dma((16,)), dma((16,)),
-            dma((F,)), dma((F,)),
+            dma((2 * F,)), dma((2 * F,)),
         ],
         compiler_params=pltpu.CompilerParams(
             collective_id=0, has_side_effects=True, vmem_limit_bytes=60 * 1024 * 1024),

time: 44.8 us -> 43.7 us (0.975)
  Pallas kernels: 43 us -> 41.9 us
    pallas_call x1, Pallas kernels: 43 us -> 41.9 us  [shards(): pl.pallas_call(kernel, out_shape=jax.ShapeDtypeStruct((2, 2, F, PATCH, C)...]
where the time goes in v3:
time: 43.7 us; the launch traced here: 43.6 us
  Pallas kernels  41.9 us (96%)
  local copies, waits for them, and re-layouts  1.67 us (4%)
    pallas_call x1, Pallas kernels, shards(): pl.pallas_call(kernel, out_shape=jax.ShapeDtypeStruct((2, 2, F, PATCH, C)...  41.9 us
    unnamed x1, local copies, waits for them, and re-layouts  1.67 us

profile of v3, /device:TPU:4, one launch (start us, length us, event | category | flops | bytes accessed | tf_op | source)
XLA Modules:
  0.0 43.6 jit_solution(11598789732024607420)
XLA Ops:
  0.0 41.9 %shard_map.100 = bf16[2,2,16,8,256]{4,3,2,1,0:T(8,128)(2,1)} custom-call(bf16[2,2,16,8,256]{4,3,2,1,0:T(8,128)(2,1)} %bitcast.10, f32[1,256]{1,0:T(1,128)} %bitcast.11, bf16[27,256,256]{2,1,0:T(8,128)(2,1)} %bitcast.7, f32[1,256]{1,0:T(1,128)} %bitcast.12, bf16[27,256,256]{2,1,0:T(8,128)(2,1)} %bitcast.8, f32[1,256]{1,0:T(1,128)} %bitcast.13, ...), custom_call_target="tpu_custom_call" | custom-call | tf_op jit(solution)/shard_map/pallas_call | solution.py:316
  42.0 1.7 %copy.12 = bf16[2,2,128,256]{3,2,1,0:T(8,128)(2,1)} copy(bf16[2,2,128,256]{3,2,1,0:T(8,128)(2,1)} %bitcast.9) | data formatting | bytes 524288

commit v4 on v3

--- a/solution.py
+++ b/solution.py
@@ -22,6 +22,11 @@
 def snake(i):
     half = i // 8
     return i + half * (23 - 2 * i)
+
+
+def band_of(r):
+    odd, x_low = (r // 4) % 2, (r // 2) % 2
+    return r + odd * (2 - 4 * x_low)
 
 
 def rms(x, gain):
@@ -124,7 +129,12 @@
     r = lax.axis_index("rows")
     g = snake(f)
     mine = f // 8
-    up, down = (r + R - 1) % R, (r + 1) % R
+    w = band_of(r)
+    moved_band = (r // 4) % 2
+    up, down = band_of((w + R - 1) % R), band_of((w + 1) % R)
+
+    def remote(peer):
+        return (peer != f) | (moved_band == 1)
     west, east = snake((g + F - 1) % F), snake((g + 1) % F)
 
     loads = [pltpu.make_async_copy(src, dst, lsem.at[n]) for n, (src, dst) in enumerate(
@@ -136,10 +146,14 @@
     barrier = pltpu.get_barrier_semaphore()
 
     def greet(k, carry):
-        pl.semaphore_signal(barrier, inc=1, device_id=((f + k) % F, r), device_id_type=MESH)
+        @pl.when(remote(k))
+        def _():
+            pl.semaphore_signal(barrier, inc=1, device_id=(k, w), device_id_type=MESH)
         return carry
 
-    lax.fori_loop(1, F, greet, 0)
+    lax.fori_loop(0, F, greet, 0)
+    for ff in (west, east):
+        pl.semaphore_signal(barrier, inc=1, device_id=(ff, r), device_id_type=MESH)
     for rr in (up, down):
         for ff in (west, f, east):
             pl.semaphore_signal(barrier, inc=1, device_id=(ff, rr), device_id_type=MESH)
@@ -160,20 +174,28 @@
     for buf in (wa_h, ea_h, wb_h, eb_h):
         for at in (0, 3):
             buf[:, at] = jnp.zeros((2, H, C), BF)
-    pl.semaphore_wait(barrier, F - 1 + 6)
+    pl.semaphore_wait(barrier, F - 1 + moved_band + 8)
     loads[0].wait()
 
     def in_copy(k, peer, source):
         return pltpu.make_async_remote_copy(
             vloc.at[:, :, snake(peer)], rin.at[source], in_send.at[k], in_recv.at[source],
-            device_id=(peer, r), device_id_type=MESH)
+            device_id=(peer, w), device_id_type=MESH)
 
     def in_start(k, carry):
-        in_copy(k, (f + k) % F, f).start()
+        peer = (f + k) % F
+
+        @pl.when(remote(peer))
+        def _():
+            in_copy(k, peer, f).start()
         return carry
 
-    lax.fori_loop(1, F, in_start, 0)
-    rin[f] = vloc[:, :, g]
+    lax.fori_loop(0, F, in_start, 0)
+
+    @pl.when(moved_band == 0)
+    def _():
+        rin[f] = vloc[:, :, g]
+
     for load in loads[1:]:
         load.wait()
 
@@ -198,20 +220,24 @@
                 device_id=to, device_id_type=MESH)
             for n, (src, dst, to) in enumerate(plan)
         ]
+        return copies
+
+    def halo_start(copies, before=()):
+        for copy in before:
+            copy.wait_send()
         for copy in copies:
             copy.start()
-        return copies
 
     def halo_end(lands, copies, h):
         for copy in copies:
-            copy.wait()
+            copy.wait_recv()
         north, south, west_h, east_h = lands
 
-        @pl.when(r == 0)
+        @pl.when(w == 0)
         def _():
             north[h] = jnp.zeros((PATCH + 2, H, C), BF)
 
-        @pl.when(r == R - 1)
+        @pl.when(w == R - 1)
         def _():
             south[h] = jnp.zeros((PATCH + 2, H, C), BF)
 
@@ -234,7 +260,7 @@
         def in_wait(k, carry):
             src = 8 * h + k
 
-            @pl.when(src != f)
+            @pl.when(remote(src))
             def _():
                 in_copy(0, src, src).wait_recv()
             return carry
@@ -245,15 +271,19 @@
         act = silu(rms(x, ga[...])).astype(BF)
         act_a[h, 1:3, 1 : PATCH + 1] = act.reshape(2, PATCH, H, C)
         halos_a.append(halo(act_a, lands_a, ha_send, ha_recv, h))
-
-    for h in range(2):
-        inner_taps(act_a, ka, ya, h)
+        if h == 0:
+            halo_start(halos_a[0])
+
+    inner_taps(act_a, ka, ya, 0)
+    halo_start(halos_a[1], halos_a[0])
+    inner_taps(act_a, ka, ya, 1)
     for h in range(2):
         halo_end(lands_a, halos_a[h], h)
         inner = edge_taps(*lands_a, ka, ya, h).astype(BF).astype(F32)
         act = silu(rms(inner, gb[...])).astype(BF)
         act_b[h, 1:3, 1 : PATCH + 1] = act.reshape(2, PATCH, H, C)
         halos_b.append(halo(act_b, lands_b, hb_send, hb_recv, h))
+        halo_start(halos_b[h], halos_b[0] if h else halos_a[1])
     for h in range(2):
         inner_taps(act_b, kb, yb, h)
 
@@ -261,7 +291,7 @@
         return pltpu.make_async_remote_copy(
             sbuf.at[dst, row], out.at[:, row, snake(source)],
             out_send.at[2 * k + row], out_recv.at[2 * source + row],
-            device_id=(dst, r), device_id_type=MESH)
+            device_id=(dst, w), device_id_type=MESH)
 
     own = [pltpu.make_async_copy(sbuf.at[f, row], out.at[:, row, g], lsem.at[row])
            for row in range(2)]
@@ -281,14 +311,14 @@
             moved = dot(perm_row[...], encoded).astype(BF)
             sbuf[8 * h : 8 * h + 8, row] = moved.reshape(8, 2, PATCH, C)
 
-            @pl.when(mine == h)
+            @pl.when((mine == h) & (moved_band == 0))
             def _():
                 own[row].start()
 
             def out_start(k, carry):
                 dst = 8 * h + k
 
-                @pl.when(dst != f)
+                @pl.when(remote(dst))
                 def _():
                     out_copy(dst, f, row, dst).start()
                 return carry
@@ -297,27 +327,35 @@
 
     def finish(k, carry):
         src = (f + k) % F
-        in_copy(k, src, src).wait_send()
-        for row in range(2):
-            out_copy(src, src, row, src).wait()
+
+        @pl.when(remote(src))
+        def _():
+            in_copy(k, src, src).wait_send()
+            for row in range(2):
+                out_copy(src, src, row, src).wait()
         return carry
 
-    lax.fori_loop(1, F, finish, 0)
-    for copy in own:
-        copy.wait()
+    lax.fori_loop(0, F, finish, 0)
+    for copy in halos_b[1]:
+        copy.wait_send()
+
+    @pl.when(moved_band == 0)
+    def _():
+        for copy in own:
+            copy.wait()
 
 
 def shards(video, na, ca, nb, cb, nc, wq, wk, wv, wo):
-    any_spec = pl.BlockSpec(memory_space=pl.ANY)
+    any_spec = pl.BlockSpec(memory_space=pltpu.HBM)
     dma = pltpu.SemaphoreType.DMA
     vm = pltpu.VMEM
     halo = (2, 4, PATCH + 2, H, C)
     lands = [vm((2, n, H, C), BF) for n in (PATCH + 2, PATCH + 2, 4, 4)]
     out = pl.pallas_call(
         kernel,
-        out_shape=jax.ShapeDtypeStruct((2, 2, F, PATCH, C), BF),
+        out_shape=pltpu.VMEM((2, 2, F, PATCH, C), BF),
         in_specs=[any_spec] * 10,
-        out_specs=any_spec,
+        out_specs=pl.BlockSpec(memory_space=pltpu.VMEM),
         scratch_shapes=[
             vm((2, 2, F, PATCH, C), BF), vm((F, 2, 2, PATCH, C), BF), vm((2, 256, C), BF),
             vm(halo, BF), vm(halo, BF), vm((27, C, C), BF), vm((27, C, C), BF),

time: 43.7 us -> 41.5 us (0.950)
  Pallas kernels: 41.9 us -> 40.7 us
  local copies, waits for them, and re-layouts: 1.67 us -> 0.71 us
    pallas_call x1, Pallas kernels: 41.9 us -> 40.7 us  [shards(): pl.pallas_call(kernel, out_shape=pltpu.VMEM((2, 2, F, PATCH, C), BF), in_...]
    unnamed x1, local copies, waits for them, and re-layouts: 1.67 us -> 0.71 us
where the time goes in v4:
time: 41.5 us; the launch traced here: 41.4 us
  Pallas kernels  40.7 us (98%)
  local copies, waits for them, and re-layouts  0.71 us (2%)
    pallas_call x1, Pallas kernels, shards(): pl.pallas_call(kernel, out_shape=pltpu.VMEM((2, 2, F, PATCH, C), BF), in_...  40.7 us

profile of v4, /device:TPU:4, one launch (start us, length us, event | category | flops | bytes accessed | tf_op | source)
XLA Modules:
  0.0 41.4 jit_solution(17588488587411555127)
XLA Ops:
  0.0 40.7 %shard_map.100 = bf16[2,2,16,8,256]{4,3,2,1,0:T(8,128)(2,1)S(1)} custom-call(bf16[2,2,16,8,256]{4,3,2,1,0:T(8,128)(2,1)} %bitcast.10, f32[1,256]{1,0:T(1,128)} %bitcast.11, bf16[27,256,256]{2,1,0:T(8,128)(2,1)} %bitcast.8, f32[1,256]{1,0:T(1,128)} %bitcast.12, bf16[27,256,256]{2,1,0:T(8,128)(2,1)} %bitcast.9, f32[1,256]{1,0:T(1,128)} %bitcast.13, ...), custom_call_target="tpu_custom_call" | custom-call | tf_op jit(solution)/shard_map/pallas_call | solution.py:354
  40.7 0.7 %copy.12 = bf16[2,2,128,256]{3,2,1,0:T(8,128)(2,1)} copy(bf16[2,2,128,256]{3,2,1,0:T(8,128)(2,1)S(1)} %bitcast.7) | data formatting | bytes 524288

commit v5 on v4

--- a/solution.py
+++ b/solution.py
@@ -88,13 +88,12 @@
     return lax.broadcasted_iota(jnp.int32, shape, dim)
 
 
-def attend_row(h, row, qs, ks, vs, att, hmask):
+def attend_row(h, row, qs, ks, vs, att, hmask, pmask):
     keys = H * (h + 1)
     group = 128 // keys
-    scale = 32 ** -0.5
+    scale = 32 ** -0.5 * 1.4426950408889634
     causal = iota((1, keys, 128), 1) <= (iota((1, keys, 128), 2) & 15) + H * h
     lane_head = iota((H, 128), 1) >> 5
-    row_pixel = iota((128, 128), 0) >> (4 + h)
     for u in range(row * 8 // group, (row + 1) * 8 // group):
         pixels = range(u * group, (u + 1) * group)
         scores = []
@@ -103,7 +102,7 @@
             scores.append(dot_tt(ks[p, 0:keys], q_bd, ((1,), (1,))))
         s = jnp.concatenate(scores, axis=0).reshape(group, keys, 128)
         s = jnp.where(causal, s, -1e30)
-        e = jnp.exp((s - jnp.max(s, axis=1, keepdims=True)) * scale)
+        e = jnp.exp2((s - jnp.max(s, axis=1, keepdims=True)) * scale)
         probs = (e * (1.0 / jnp.sum(e, axis=1, keepdims=True))).astype(BF)
         probs = probs.reshape(128, 128).T
         value = vs[pl.ds(u * group, group), 0:keys].reshape(128, C)
@@ -111,7 +110,7 @@
             lanes = slice(128 * hh, 128 * hh + 128)
             part = value[:, lanes]
             v_bd = jnp.concatenate(
-                [part * (row_pixel == n).astype(BF) for n in range(group)], axis=1)
+                [part * pmask[8 * h + n] for n in range(group)], axis=1)
             o = dot(probs[64 * hh : 64 * hh + 64], v_bd)
             for n, p in enumerate(pixels):
                 tile = o[:, 128 * n : 128 * n + 128]
@@ -123,7 +122,7 @@
 
 def kernel(video, na, ca, nb, cb, nc, wq, wk, wv, wo, out,
            vloc, rin, xres, act_a, act_b, ka, kb, ga, gb, gc, sq, sk, sv, so,
-           perm, perm_row, hmask, ya, yb, na_h, sa_h, wa_h, ea_h, nb_h, sb_h, wb_h, eb_h, qs, ks, vs, att, blk, sbuf,
+           perm, perm_row, hmask, pmask, ya, yb, na_h, sa_h, wa_h, ea_h, nb_h, sb_h, wb_h, eb_h, qs, ks, vs, att, blk, sbuf,
            lsem, in_send, in_recv, ha_send, ha_recv, hb_send, hb_recv, out_send, out_recv):
     f = lax.axis_index("frames")
     r = lax.axis_index("rows")
@@ -164,6 +163,11 @@
         (iota((128, C), 0) >> 4) == (iota((128, C), 1) >> 5), 1.0, 0.0).astype(BF)
     a, b = iota((128, 128), 0), iota((128, 128), 1)
     perm_row[...] = jnp.where(b == ((a & 7) << 4) + (a >> 3), 1.0, 0.0).astype(BF)
+    row_at = iota((128, 128), 0)
+    for n in range(8):
+        pmask[n] = jnp.where((row_at >> 4) == n, 1.0, 0.0).astype(BF)
+    for n in range(4):
+        pmask[8 + n] = jnp.where((row_at >> 5) == n, 1.0, 0.0).astype(BF)
     for ys in (ya, yb):
         ys[:, :, 0:8] = jnp.zeros((3, 16, 8, C), F32)
     for buf in (act_a, act_b):
@@ -303,8 +307,11 @@
         qs[h] = dot(normed, sq[...]).astype(BF).reshape(16, H, C)
         ks[:, H * h : H * h + H] = dot(normed, sk[...]).astype(BF).reshape(16, H, C)
         vs[:, H * h : H * h + H] = dot(normed, sv[...]).astype(BF).reshape(16, H, C)
+        for row in range(2 if h == 0 else 0):
+            attend_row(h, row, qs, ks, vs, att, hmask, pmask)
         for row in range(2):
-            attend_row(h, row, qs, ks, vs, att, hmask)
+            if h == 1:
+                attend_row(h, row, qs, ks, vs, att, hmask, pmask)
             at = slice(128 * row, 128 * row + 128)
             projected = dot(att[8 * row : 8 * row + 8].reshape(128, C), so[...])
             encoded = (blk[at].astype(F32) + projected.astype(BF).astype(F32)).astype(BF)
@@ -361,7 +368,7 @@
             vm(halo, BF), vm(halo, BF), vm((27, C, C), BF), vm((27, C, C), BF),
             vm((1, C), F32), vm((1, C), F32), vm((1, C), F32),
             vm((C, C), BF), vm((C, C), BF), vm((C, C), BF), vm((C, C), BF),
-            vm((256, 256), BF), vm((128, 128), BF), vm((128, C), BF),
+            vm((256, 256), BF), vm((128, 128), BF), vm((128, C), BF), vm((12, 128, 128), BF),
             vm((3, 16, 40, C), F32), vm((3, 16, 40, C), F32),
             *lands, *lands,
             vm((2, 16, H, C), BF), vm((16, T, C), BF), vm((16, T, C), BF), vm((16, H, C), BF),

time: 41.5 us -> 41.3 us (level)
  no operation moved by 1% of the time
where the time goes in v5:
time: 41.3 us; the launch traced here: 41.2 us
  Pallas kernels  40.5 us (98%)
  local copies, waits for them, and re-layouts  0.71 us (2%)
    pallas_call x1, Pallas kernels, shards(): pl.pallas_call(kernel, out_shape=pltpu.VMEM((2, 2, F, PATCH, C), BF), in_...  40.5 us

profile of v5, /device:TPU:4, one launch (start us, length us, event | category | flops | bytes accessed | tf_op | source)
XLA Modules:
  0.0 41.2 jit_solution(463256074311379854)
XLA Ops:
  0.0 40.5 %shard_map.100 = bf16[2,2,16,8,256]{4,3,2,1,0:T(8,128)(2,1)S(1)} custom-call(bf16[2,2,16,8,256]{4,3,2,1,0:T(8,128)(2,1)} %bitcast.10, f32[1,256]{1,0:T(1,128)} %bitcast.11, bf16[27,256,256]{2,1,0:T(8,128)(2,1)} %bitcast.8, f32[1,256]{1,0:T(1,128)} %bitcast.12, bf16[27,256,256]{2,1,0:T(8,128)(2,1)} %bitcast.9, f32[1,256]{1,0:T(1,128)} %bitcast.13, ...), custom_call_target="tpu_custom_call" | custom-call | tf_op jit(solution)/shard_map/pallas_call | solution.py:361
  40.5 0.7 %copy.12 = bf16[2,2,128,256]{3,2,1,0:T(8,128)(2,1)} copy(bf16[2,2,128,256]{3,2,1,0:T(8,128)(2,1)S(1)} %bitcast.7) | data formatting | bytes 524288

commit v6 on v5

--- a/solution.py
+++ b/solution.py
@@ -136,18 +136,14 @@
         return (peer != f) | (moved_band == 1)
     west, east = snake((g + F - 1) % F), snake((g + 1) % F)
 
-    loads = [pltpu.make_async_copy(src, dst, lsem.at[n]) for n, (src, dst) in enumerate(
-        [(video, vloc), (na, ga), (ca, ka), (nb, gb), (cb, kb), (nc, gc),
-         (wq, sq), (wk, sk), (wv, sv), (wo, so)])]
-    for load in loads:
-        load.start()
-
     barrier = pltpu.get_barrier_semaphore()
 
     def greet(k, carry):
-        @pl.when(remote(k))
-        def _():
-            pl.semaphore_signal(barrier, inc=1, device_id=(k, w), device_id_type=MESH)
+        peer = (f + 4 + k) % F
+
+        @pl.when(remote(peer))
+        def _():
+            pl.semaphore_signal(barrier, inc=1, device_id=(peer, w), device_id_type=MESH)
         return carry
 
     lax.fori_loop(0, F, greet, 0)
@@ -156,6 +152,12 @@
     for rr in (up, down):
         for ff in (west, f, east):
             pl.semaphore_signal(barrier, inc=1, device_id=(ff, rr), device_id_type=MESH)
+
+    loads = [pltpu.make_async_copy(src, dst, lsem.at[n]) for n, (src, dst) in enumerate(
+        [(video, vloc), (na, ga), (ca, ka), (nb, gb), (cb, kb), (nc, gc),
+         (wq, sq), (wk, sk), (wv, sv), (wo, so)])]
+    for load in loads:
+        load.start()
 
     a, b = iota((256, 256), 0), iota((256, 256), 1)
     perm[...] = jnp.where(b == ((a & 15) << 4) + (a >> 4), 1.0, 0.0).astype(BF)

time: 41.3 us -> 41.4 us (level)
  no operation moved by 1% of the time
where the time goes in v6:
time: 41.4 us; the launch traced here: 41.3 us
  Pallas kernels  40.6 us (98%)
  local copies, waits for them, and re-layouts  0.71 us (2%)
    pallas_call x1, Pallas kernels, shards(): pl.pallas_call(kernel, out_shape=pltpu.VMEM((2, 2, F, PATCH, C), BF), in_...  40.6 us

profile of v6, /device:TPU:4, one launch (start us, length us, event | category | flops | bytes accessed | tf_op | source)
XLA Modules:
  0.0 41.3 jit_solution(16855227913857918208)
XLA Ops:
  0.0 40.6 %shard_map.100 = bf16[2,2,16,8,256]{4,3,2,1,0:T(8,128)(2,1)S(1)} custom-call(bf16[2,2,16,8,256]{4,3,2,1,0:T(8,128)(2,1)} %bitcast.10, f32[1,256]{1,0:T(1,128)} %bitcast.11, bf16[27,256,256]{2,1,0:T(8,128)(2,1)} %bitcast.8, f32[1,256]{1,0:T(1,128)} %bitcast.12, bf16[27,256,256]{2,1,0:T(8,128)(2,1)} %bitcast.9, f32[1,256]{1,0:T(1,128)} %bitcast.13, ...), custom_call_target="tpu_custom_call" | custom-call | tf_op jit(solution)/shard_map/pallas_call | solution.py:363
  40.6 0.7 %copy.12 = bf16[2,2,128,256]{3,2,1,0:T(8,128)(2,1)} copy(bf16[2,2,128,256]{3,2,1,0:T(8,128)(2,1)S(1)} %bitcast.7) | data formatting | bytes 524288
